TPU v7x, 32 devices: a whole 2x2x4 slice. The times are simulated.
32 devices in a mesh: gx: 4 (over y, x), gy: 2 (over core), gz: 4 (over z).
Axes of the slice: x: 2, y: 2, z: 4, core: 2. Of those that a mesh axis runs over, the one named last changes fastest.
Arguments:
- flow_state: float32 [5, 128, 32, 512], P(None, 'gz', 'gy', 'gx'), may hold values from -5 to 120, as said below
- advection: float32 [3, 5], replicated, may hold values from -400 to 400, as said below
- inverse_x: float32 [5, 128, 128], replicated, may hold values from -1 to 1, as said below
- inverse_y: float32 [5, 16, 16], replicated, may hold values from -1 to 1, as said below
- inverse_z: float32 [5, 32, 32], replicated, may hold values from -1 to 1, as said below
- reduced_x: float32 [5, 16, 16], replicated, as said below
- reduced_y: float32 [5, 8, 8], replicated, as said below
- reduced_z: float32 [5, 16, 16], replicated, as said below
Outputs:
- update: float32 [5, 128, 32, 512], P(None, 'gz', 'gy', 'gx')
- rms_norm: float32 [5], replicated
Inputs may be any that keep to these rules, and one draw needn't show every extreme that they name: flow_state[0] (density) lies between 0.5 and 2, and flow_state[4] / density minus half the squared velocity is at least 0.6 in every cell. `advection`: every entry has magnitude between 100 and 400. inverse_x[v] is the inverse of the 128 x 128 matrix with 4 on the diagonal, advection[0, v] / 2 - 2 just above it, -advection[0, v] / 2 - 2 just below it and 0.5 two places off it. inverse_y[v] is the inverse of the 16 x 16 matrix built likewise from advection[1, v]. inverse_z[v] is the inverse of the 32 x 32 matrix built likewise from advection[2, v]. reduced_x[v] is the inverse of I + K, K being the boundary rows and columns of the block inverses times the coupling between blocks, so that S_x equals the exact solution of the banded system along whole x lines with nothing beyond the grid's ends. reduced_y[v] is built likewise for y lines. reduced_z[v] is built likewise for z lines.
All inputs are finite; a program needn't handle non-finite values.
Results may differ from a plain program's by a relative error of at most 0.0002.
Values sent between devices are 32-bit elements.
A program may use at most 64 MiB of HBM per device.

v0:
```python
import jax
import jax.numpy as jnp
import numpy as np
from jax import lax
from jax.sharding import PartitionSpec as P

exact_mode = lax.Precision.HIGHEST
gas_ratio = 0.4
courant = 8000.0
damping = 0.0625
fourth_coef = 0.5


def with_halo(block, sides, width):
    for axis, dim in sides:
        count = lax.axis_size(axis)
        forward = [(i, i + 1) for i in range(count - 1)]
        forward.append((count - 1, 0))
        backward = [(target, source) for source, target in forward]
        low = lax.ppermute(
            lax.slice_in_dim(block, block.shape[dim] - width, None, axis=dim), axis, forward
        )
        high = lax.ppermute(lax.slice_in_dim(block, 0, width, axis=dim), axis, backward)
        block = jnp.concatenate([low, block, high], axis=dim)
    return block


def primitives(flow_state):
    density = flow_state[0]
    velocity = flow_state[1:4] / density
    kinetic = 0.5 * jnp.sum(velocity * velocity, axis=0)
    internal = jnp.maximum(flow_state[4] / density - kinetic, 0.25)
    pressure = gas_ratio * density * internal
    return (velocity, internal, pressure)


def fluxes_along(flow_state, direction):
    velocity, internal, pressure = primitives(flow_state)
    carried = velocity[direction]
    columns = [flow_state[1 + direction]]
    for component in range(3):
        moment = flow_state[1 + component] * carried
        if component == direction:
            moment = moment + pressure
        columns.append(moment)
    columns.append((flow_state[4] + pressure) * carried)
    return jnp.stack(columns)


def window(padded, line_axis, offset, margin):
    slices = [slice(None), slice(2, -2), slice(2, -2), slice(2, -2)]
    extent = padded.shape[line_axis] - 4
    slices[line_axis] = slice(2 + offset - margin, 2 + offset + extent + margin)
    return padded[tuple(slices)]


def residual_field(padded):
    centre = window(padded, 1, 0, 0)
    running = jnp.zeros_like(centre)
    for direction in range(3):
        line_axis = 3 - direction
        fluxes = fluxes_along(window(padded, line_axis, 0, 1), direction)
        extent = fluxes.shape[line_axis]
        forward = lax.slice_in_dim(fluxes, 2, extent, axis=line_axis)
        backward = lax.slice_in_dim(fluxes, 0, extent - 2, axis=line_axis)
        running = running - 0.5 * (forward - backward)
        fourth = (
            window(padded, line_axis, -2, 0)
            - 4.0 * window(padded, line_axis, -1, 0)
            + 6.0 * centre
            - 4.0 * window(padded, line_axis, 1, 0)
            + window(padded, line_axis, 2, 0)
        )
        running = running - damping * fourth
    return running


def neighbour_table(reduced):
    blocks = reduced.shape[1] // 4
    padded = jnp.pad(reduced, ((0, 0), (2, 2), (0, 0)))
    picked = (4 * np.arange(blocks)[:, None] + np.array([0, 1, 6, 7])[None, :]).reshape(-1)
    return jnp.transpose(padded[:, picked, :], (1, 0, 2))


def gather_terms(own_rows, carry, piece):
    columns = lax.slice_in_dim(own_rows, 0, piece.shape[1], axis=2)
    return carry + jnp.einsum("rvq,vqn->rvn", columns, piece, precision=exact_mode)


def empty_rows(boundary_rows):
    return jnp.zeros((4, boundary_rows.shape[0], boundary_rows.shape[2]), jnp.float32)


def line_solve(line_field, line_axis, inverse, speeds, nearby):
    block_len = inverse.shape[1]
    patterns = {3: "vij,vzyj->vzyi", 2: "vij,vzjx->vzix", 1: "vij,vjyx->viyx"}
    local_part = jnp.einsum(patterns[line_axis], inverse, line_field, precision=exact_mode)
    boundary = jnp.concatenate(
        [
            lax.slice_in_dim(local_part, 0, 2, axis=line_axis),
            lax.slice_in_dim(local_part, block_len - 2, block_len, axis=line_axis),
        ],
        axis=line_axis,
    )
    boundary_rows = jnp.moveaxis(boundary, line_axis, 1)
    boundary_rows = boundary_rows.reshape(boundary_rows.shape[0], 4, -1)
    nearby_rows = nearby(boundary_rows)
    flat_shape = list(line_field.shape)
    flat_shape[line_axis] = 1
    pieces = [nearby_rows[position].reshape(flat_shape) for position in range(4)]
    factor = speeds.reshape(-1, 1, 1, 1)
    lower_one = -0.5 * factor - 4.0 * fourth_coef
    upper_one = 0.5 * factor - 4.0 * fourth_coef
    left_first = fourth_coef * pieces[0] + lower_one * pieces[1]
    left_second = fourth_coef * pieces[1]
    right_first = fourth_coef * pieces[2]
    right_second = upper_one * pieces[2] + fourth_coef * pieces[3]
    column_shape = [inverse.shape[0], 1, 1, 1]
    column_shape[line_axis] = block_len

    def column(place):
        return inverse[:, :, place].reshape(column_shape)

    correction = (
        column(0) * left_first
        + column(1) * left_second
        + column(block_len - 2) * right_first
        + column(block_len - 1) * right_second
    )
    return local_part - correction


def shards(flow_state, advection, inverse_x, inverse_y, inverse_z, reduced_x, reduced_y, reduced_z):
    velocity, internal, pressure = primitives(flow_state)
    wave_speed = jnp.sum(jnp.abs(velocity), axis=0) + jnp.sqrt(3.0 * 1.4 * gas_ratio * internal)
    local_top = jnp.max(wave_speed)
    top_speed = lax.pmax(local_top, ("gx", "gy", "gz"))
    padded = with_halo(flow_state, (("gx", 3), ("gy", 2), ("gz", 1)), 2)
    residual = residual_field(padded)
    local_sums = jnp.sum(residual * residual, axis=(1, 2, 3))
    squares = lax.psum(local_sums, ("gx", "gy", "gz"))
    cell_count = (
        residual.shape[1]
        * residual.shape[2]
        * residual.shape[3]
        * lax.axis_size("gx")
        * lax.axis_size("gy")
        * lax.axis_size("gz")
    )
    rms_norm = jnp.sqrt(squares / float(cell_count))
    time_step = courant / top_speed
    table_x = neighbour_table(reduced_x)
    table_y = neighbour_table(reduced_y)
    table_z = neighbour_table(reduced_z)
    index_x = lax.axis_index("gx")
    index_y = lax.axis_index("gy")
    index_z = lax.axis_index("gz")

    def nearby_x(boundary_rows):
        own_rows = lax.dynamic_slice_in_dim(table_x, 4 * index_x, 4, 0)
        return gather_terms(
            own_rows,
            empty_rows(boundary_rows),
            lax.all_gather(boundary_rows, "gx", axis=1, tiled=True),
        )

    def nearby_y(boundary_rows):
        own_rows = lax.dynamic_slice_in_dim(table_y, 4 * index_y, 4, 0)
        return gather_terms(
            own_rows,
            empty_rows(boundary_rows),
            lax.all_gather(boundary_rows, "gy", axis=1, tiled=True),
        )

    def nearby_z(boundary_rows):
        own_rows = lax.dynamic_slice_in_dim(table_z, 4 * index_z, 4, 0)
        return gather_terms(
            own_rows,
            empty_rows(boundary_rows),
            lax.all_gather(boundary_rows, "gz", axis=1, tiled=True),
        )

    line_field = time_step * residual
    line_field = line_solve(line_field, 3, inverse_x, advection[0], nearby_x)
    line_field = line_solve(line_field, 2, inverse_y, advection[1], nearby_y)
    line_field = line_solve(line_field, 1, inverse_z, advection[2], nearby_z)
    return (line_field, rms_norm)


def solution(mesh):
    placed = (P(None, "gz", "gy", "gx"), P(), P(), P(), P(), P(), P(), P())
    return jax.shard_map(
        shards,
        mesh=mesh,
        in_specs=placed,
        out_specs=(P(None, "gz", "gy", "gx"), P()),
        check_vma=False,
    )
```

profile of v0, /device:TPU:0, one launch (start us, length us, event | category | flops | bytes accessed | tf_op | source)
XLA Modules:
  0.0 199.7 jit_solution(9656226875409152906)
XLA Ops:
  0.6 3.4 %fusion.82 = (f32[5,32,16,2]{3,2,1,0:T(8,128)}, f32[5,32,16,2]{3,2,1,0:T(8,128)S(1)}) fusion(f32[5,32,16,128]{3,2,1,0:T(8,128)} %param.14), kind=kLoop, calls=%fused_computation.201 | loop fusion | bytes 81920 | tf_op jit(solution)/shard_map/slice | solution.py:21
  4.0 2.6 %copy.172 = f32[5,32,16,2]{1,2,3,0:T(8,128)} copy(f32[5,32,16,2]{3,2,1,0:T(8,128)} %get-tuple-element.48) | data formatting | bytes 40960
  6.6 3.0 %collective-permute-start = (f32[5,32,16,2]{1,2,3,0:T(8,128)}, f32[5,32,16,2]{1,2,3,0:T(8,128)}, u32[]{:S(2)}, u32[]{:S(2)}) collective-permute-start(f32[5,32,16,2]{1,2,3,0:T(8,128)} %copy.172), channel_id=1, source_target_pairs={{0,8},{8,16},{16,24},{24,0},{1,9},{9,17},{17,25},{25,1},{2,10},{10... | collective-permute-start | bytes 61448 | tf_op jit(solution)/shard_map/ppermute | solution.py:20
  9.6 1.3 copy.173
  10.9 1.0 collective-permute-start.1
  12.0 0.6 copy.143
  12.7 0.6 add_bitcast_fusion.1
  13.3 0.3 fusion.83
  13.6 0.7 copy.151
  14.3 1.5 pad.11
  15.8 0.6 pad.12
  16.4 1.7 fusion.85
  18.1 0.8 copy.160
  18.9 0.6 pad.13
  19.5 1.3 pad_clamp_fusion
  20.8 2.2 %gather_fusion = f32[16,5,16]{2,1,0:T(8,128)} fusion(f32[5,20,16]{2,0,1:T(8,128)} %pad.11, s32[1024]{0:T(1024)} %get-tuple-element.89), kind=kCustom, calls=%fused_computation | custom fusion | bytes 10304 | tf_op jit(solution)/shard_map/gather | solution.py:82
  23.0 2.2 %gather_fusion.2 = f32[16,5,16]{2,1,0:T(8,128)} fusion(f32[5,20,16]{2,0,1:T(8,128)} %pad.13, s32[1024]{0:T(1024)} %get-tuple-element.89), kind=kCustom, calls=%fused_computation.2 | custom fusion | bytes 10304 | tf_op jit(solution)/shard_map/gather | solution.py:82
  25.2 0.8 fusion.84
  26.0 0.7 fusion.68
  26.7 0.7 constant_dynamic-slice_fusion.2
  27.5 1.5 gather_fusion.1
  29.0 0.7 constant_dynamic-slice_fusion
  29.7 40.3 %pmax.7 = f32[]{:T(128)} all-reduce(f32[]{:T(128)} %fusion.68), channel_id=1, replica_groups=mesh['gx'=4,'gy'=2,'gz'=4] {'gx','gy','gz'}, use_global_device_ids=true, to_apply=%region_3.0 | all-reduce | flops 1 | bytes 8 | tf_op jit(solution)/shard_map/pmax | solution.py:137
  70.0 1.5 copy.124
  73.9 1.4 copy.123
  75.4 1.4 copy.125
  76.8 2.4 %pad_maximum_fusion.1 = f32[5,32,16,132]{3,1,2,0:T(8,128)S(1)} fusion(f32[5,32,16,2]{3,1,2,0:T(8,128)S(1)} %copy.125, f32[5,32,16,128]{3,1,2,0:T(8,128)} %copy.124, f32[5,32,16,2]{3,1,2,0:T(8,128)S(1)} %copy.123), kind=kLoop, calls=%fused_computation.5 | loop fusion | flops 675840 | bytes 2703360 | tf_op jit(solution)/shard_map/concatenate | solution.py:24
  79.2 0.3 slice_bitcast_fusion
  79.6 0.5 multiply_reduce_fusion
  80.1 0.5 add_dynamic-update-slice_fusion
  81.1 0.5 collective-permute-start.3
  81.6 0.3 multiply_dynamic-update-slice_fusion
  82.0 0.8 collective-permute-done.2
  82.7 0.5 collective-permute-done.3
  83.2 0.6 pad_maximum_fusion.32
  83.8 1.6 collective-permute-start.4
  85.4 2.6 %collective-permute-start.5 = (f32[5,2,20,132]{3,2,1,0:T(8,128)S(1)}, f32[5,2,20,132]{3,2,1,0:T(8,128)S(1)}, u32[]{:S(2)}, u32[]{:S(2)}) collective-permute-start(f32[5,2,20,132]{3,2,1,0:T(8,128)S(1)} %copy.132), channel_id=1, source_target_pairs={{1,0},{2,1},{3,2},{0,3},{5,4},{6,5},{7,6},{4,7},{9,8},{10,9},{11,1... | collective-permute-start | bytes 316808 | tf_op jit(solution)/shard_map/ppermute | solution.py:23
  88.2 1.1 pad_maximum_fusion
  89.3 0.3 multiply_reduce_fusion.3
  89.7 0.2 add_dynamic-update-slice_fusion.2
  90.3 4.3 %collective-permute-done.4 = f32[5,2,20,132]{3,2,1,0:T(8,128)S(1)} collective-permute-done((f32[5,2,20,132]{3,2,1,0:T(8,128)S(1)}, f32[5,2,20,132]{3,2,1,0:T(8,128)S(1)}, u32[]{:S(2)}, u32[]{:S(2)}) %collective-permute-start.4) | collective-permute-done | bytes 105632 | tf_op jit(solution)/shard_map/ppermute | solution.py:20
  94.6 4.0 %collective-permute-done.5 = f32[5,2,20,132]{3,2,1,0:T(8,128)S(1)} collective-permute-done((f32[5,2,20,132]{3,2,1,0:T(8,128)S(1)}, f32[5,2,20,132]{3,2,1,0:T(8,128)S(1)}, u32[]{:S(2)}, u32[]{:S(2)}) %collective-permute-start.5) | collective-permute-done | bytes 105632 | tf_op jit(solution)/shard_map/ppermute | solution.py:23
  98.7 0.3 constant_dynamic-update-slice_fusion.1
  99.0 0.5 multiply_reduce_fusion.2
  100.0 0.3 add_dynamic-update-slice_fusion.1
  100.4 7.5 %multiply_reduce_fusion.1 = (f32[5]{0:T(128)S(1)}, f32[5,32,16,128]{3,1,2,0:T(8,128)S(1)}) fusion(f32[5,2,20,132]{3,1,2,0:T(2,128)S(1)} %copy.134, f32[5,32,2,132]{3,1,2,0:T(8,128)S(1)} %collective-permute-done.3, f32[5,32,16,2]{3,1,2,0:T(8,128)S(1)} %copy.125, f32[5,32,16,128]{3,1,2,0:T(8,128)S(1)} %copy-done, f32[5,32,16,2]{3,1,2,0:T(8,128)S(1)} %copy.123, ...), kind=kLoop, calls=%fused_computation.71 | loop fusion | flops 23592956 | bytes 11075860 | tf_op jit(solution)/shard_map/reduce_sum | solution.py:140
  108.0 2.1 %fusion.30 = f32[5,32,16,128]{3,2,1,0:T(8,128)S(1)} fusion(f32[5,32,16,128]{3,1,2,0:T(8,128)S(1)} %broadcast_multiply_fusion, f32[5,128,128]{2,1,0:T(8,128)S(1)} %copy-done.2), kind=kOutput, calls=%fused_computation.69 | convolution fusion | flops 503316480 | bytes 2949120 | tf_op jit(solution)/shard_map/vij,vzyj->vzyi/dot_general | solution.py:97
  110.2 1.5 fusion.81
  111.7 1.9 copy.139
  113.6 0.6 copy.140
  114.6 9.9 %all_gather.9 = f32[5,16,512]{2,0,1:T(8,128)S(1)} all-gather(f32[5,4,512]{2,0,1:T(8,128)S(1)} %reshape.325), channel_id=1, replica_groups=mesh['gx'=4,'gy'=2,'gz'=4] {'gx'}, dimensions={1}, use_global_device_ids=true | all-gather | bytes 204800 | tf_op jit(solution)/shard_map/all_gather | solution.py:164
  124.5 0.3 convolution_bitcast_fusion.4
  125.5 3.4 %convolution_bitcast_fusion.3 = f32[5,32,16,128]{3,2,1,0:T(8,128)S(1)} fusion(f32[5,32,16,128]{3,2,1,0:T(8,128)S(1)} %fusion.30, f32[5,32,16]{2,1,0:T(8,128)S(1)} %get-tuple-element.73, f32[5,128]{1,0:T(8,128)S(1)} %bitcast.142, f32[5,32,16]{2,1,0:T(8,128)S(1)} %get-tuple-element.72, f32[5,128]{1,0:T(8,128)S(1)} %bitcast.141, ...), kind=kOutput, calls=%fused_computation.14 | convolution fusion | flops 65536000 | bytes 2677760 | tf_op jit(solution)/shard_map/vij,vzjx->vzix/dot_general | solution.py:97
  129.4 2.8 %all_gather.10 = f32[5,8,4096]{2,0,1:T(8,128)S(1)} all-gather(f32[5,4,4096]{2,0,1:T(8,128)S(1)} %copy.150), channel_id=1, replica_groups=mesh['gx'=4,'gy'=2,'gz'=4] {'gy'}, dimensions={1}, use_global_device_ids=true | all-gather | bytes 983040 | tf_op jit(solution)/shard_map/all_gather | solution.py:172
  132.1 1.1 convolution_bitcast_fusion
  133.2 0.3 slice_multiply_fusion.3
  133.7 0.5 add_subtract_fusion.1
  134.2 1.7 convolution_bitcast_fusion.2
  136.2 21.7 %all_gather.11 = f32[5,16,2048]{2,0,1:T(8,128)S(1)} all-gather(f32[5,4,2048]{2,0,1:T(8,128)S(1)} %copy.159), channel_id=1, replica_groups=mesh['gx'=4,'gy'=2,'gz'=4] {'gz'}, dimensions={1}, use_global_device_ids=true | all-gather | bytes 819200 | tf_op jit(solution)/shard_map/all_gather | solution.py:180
  157.9 0.8 convolution_bitcast_fusion.1
  159.0 0.6 add_subtract_fusion
  159.6 1.8 copy.166
  161.4 37.8 %psum.7 = f32[5]{0:T(128)S(1)} all-reduce(f32[5]{0:T(128)S(1)} %get-tuple-element.18), channel_id=1, replica_groups=mesh['gx'=4,'gy'=2,'gz'=4] {'gx','gy','gz'}, use_global_device_ids=true, to_apply=%region_8.0 | all-reduce | flops 5 | bytes 40 | tf_op jit(solution)/shard_map/psum | solution.py:141
  199.2 0.5 multiply_sqrt_fusion
  (96 shorter events, 6.2 us)
Async XLA Ops:
  4.0 7.8 %copy-start.1 = (f32[5,32,16,128]{3,2,1,0:T(8,128)S(1)}, f32[5,32,16,128]{3,2,1,0:T(8,128)}, u32[]{:S(2)}) copy-start(f32[5,32,16,128]{3,2,1,0:T(8,128)} %param.14) | copy-start | bytes 3932164
  6.6 67.3 %collective-permute-start = (f32[5,32,16,2]{1,2,3,0:T(8,128)}, f32[5,32,16,2]{1,2,3,0:T(8,128)}, u32[]{:S(2)}, u32[]{:S(2)}) collective-permute-start(f32[5,32,16,2]{1,2,3,0:T(8,128)} %copy.172), channel_id=1, source_target_pairs={{0,8},{8,16},{16,24},{24,0},{1,9},{9,17},{17,25},{25,1},{2,10},{10... | collective-permute-start | bytes 61448 | tf_op jit(solution)/shard_map/ppermute | solution.py:20
  10.9 1.2 copy-start.13
  10.9 1.8 copy-start.20
  10.9 2.4 %copy-start.2 = (f32[5,128,128]{2,1,0:T(8,128)S(1)}, f32[5,128,128]{2,1,0:T(8,128)}, u32[]{:S(2)}) copy-start(f32[5,128,128]{2,1,0:T(8,128)} %param.16) | copy-start | bytes 983044
  10.9 64.5 %collective-permute-start.1 = (f32[5,32,16,2]{1,2,3,0:T(8,128)}, f32[5,32,16,2]{1,2,3,0:T(8,128)}, u32[]{:S(2)}, u32[]{:S(2)}) collective-permute-start(f32[5,32,16,2]{1,2,3,0:T(8,128)} %copy.173), channel_id=1, source_target_pairs={{8,0},{16,8},{24,16},{0,24},{9,1},{17,9},{25,17},{1,25},{10,2},{18... | collective-permute-start | bytes 61448 | tf_op jit(solution)/shard_map/ppermute | solution.py:23
  13.3 11.9 %copy-start.3 = (f32[5,32,32]{2,1,0:T(8,128)S(1)}, f32[5,32,32]{2,1,0:T(8,128)}, u32[]{:S(2)}) copy-start(f32[5,32,32]{2,1,0:T(8,128)} %param.18) | copy-start | bytes 61444
  71.4 0.8 copy-start.12
  71.4 0.9 copy-start.11
  71.4 1.1 copy-start.10
  71.4 1.2 copy-start.9
  71.4 1.3 copy-start.8
  71.4 1.4 copy-start.7
  71.4 1.5 copy-start.6
  71.5 1.6 copy-start.5
  81.0 1.7 collective-permute-start.2
  81.1 2.1 %copy-start = (f32[5,32,16,128]{3,1,2,0:T(8,128)S(1)}, f32[5,32,16,128]{3,1,2,0:T(8,128)}, u32[]{:S(2)}) copy-start(f32[5,32,16,128]{3,1,2,0:T(8,128)} %copy.124) | copy-start | bytes 3932164
  81.1 2.1 %collective-permute-start.3 = (f32[5,32,2,132]{3,1,2,0:T(8,128)S(1)}, f32[5,32,2,132]{3,1,2,0:T(8,128)S(1)}, u32[]{:S(2)}, u32[]{:S(2)}) collective-permute-start(f32[5,32,2,132]{3,1,2,0:T(8,128)S(1)} %get-tuple-element.41), channel_id=1, source_target_pairs={{4,0},{0,4},{5,1},{1,5},{6,2},{2,6},{7,3},{3,7},{12,8},{8,12},{13,... | collective-permute-start | bytes 506888 | tf_op jit(solution)/shard_map/ppermute | solution.py:23
  83.8 10.7 %collective-permute-start.4 = (f32[5,2,20,132]{3,2,1,0:T(8,128)S(1)}, f32[5,2,20,132]{3,2,1,0:T(8,128)S(1)}, u32[]{:S(2)}, u32[]{:S(2)}) collective-permute-start(f32[5,2,20,132]{3,2,1,0:T(8,128)S(1)} %copy.131), channel_id=1, source_target_pairs={{0,1},{1,2},{2,3},{3,0},{4,5},{5,6},{6,7},{7,4},{8,9},{9,10},{10,1... | collective-permute-start | bytes 316808 | tf_op jit(solution)/shard_map/ppermute | solution.py:20
  85.4 13.2 %collective-permute-start.5 = (f32[5,2,20,132]{3,2,1,0:T(8,128)S(1)}, f32[5,2,20,132]{3,2,1,0:T(8,128)S(1)}, u32[]{:S(2)}, u32[]{:S(2)}) collective-permute-start(f32[5,2,20,132]{3,2,1,0:T(8,128)S(1)} %copy.132), channel_id=1, source_target_pairs={{1,0},{2,1},{3,2},{0,3},{5,4},{6,5},{7,6},{4,7},{9,8},{10,9},{11,1... | collective-permute-start | bytes 316808 | tf_op jit(solution)/shard_map/ppermute | solution.py:23
  114.2 11.1 %copy-start.19 = (f32[5]{0:T(128)S(1)}, f32[5]{0:T(128)}, u32[]{:S(2)}) copy-start(f32[5]{0:T(128)} %get-tuple-element.86) | copy-start | bytes 64
  114.2 11.2 %copy-start.18 = (f32[5]{0:T(128)S(1)}, f32[5]{0:T(128)}, u32[]{:S(2)}) copy-start(f32[5]{0:T(128)} %get-tuple-element.83) | copy-start | bytes 64
  114.2 11.3 %copy-start.4 = (f32[5,16,16]{2,1,0:T(8,128)S(1)}, f32[5,16,16]{2,1,0:T(8,128)}, u32[]{:S(2)}) copy-start(f32[5,16,16]{2,1,0:T(8,128)} %param.17) | copy-start | bytes 15364
  129.4 4.2 %copy-start.17 = (f32[5]{0:T(128)S(1)}, f32[5]{0:T(128)}, u32[]{:S(2)}) copy-start(f32[5]{0:T(128)} %get-tuple-element.87) | copy-start | bytes 64
  132.1 1.5 copy-start.16
  136.2 22.7 %copy-start.15 = (f32[5]{0:T(128)S(1)}, f32[5]{0:T(128)}, u32[]{:S(2)}) copy-start(f32[5]{0:T(128)} %get-tuple-element.82) | copy-start | bytes 64
  136.2 22.8 %copy-start.14 = (f32[5]{0:T(128)S(1)}, f32[5]{0:T(128)}, u32[]{:S(2)}) copy-start(f32[5]{0:T(128)} %get-tuple-element.85) | copy-start | bytes 64
where the time goes:
time: 201 us; the launch traced here: 200 us
  blocking collectives  112 us (56%)
  local copies, waits for them, and re-layouts  36.1 us (18%)
  other arithmetic  21.9 us (11%)
  waiting for transfers between devices  9.47 us (5%)
  matrix products  9.39 us (5%)
  starting transfers between devices  8.59 us (4%)
    pmax x1, blocking collectives, shards(): top_speed = lax.pmax(local_top, ('gx', 'gy', 'gz'))  40.3 us
    psum x1, blocking collectives, shards(): squares = lax.psum(local_sums, ('gx', 'gy', 'gz'))  37.8 us
    all_gather x1, blocking collectives, nearby_z(): lax.all_gather(boundary_rows, 'gz', axis=1, tiled=True)  21.7 us
    unnamed x61, local copies, waits for them, and re-layouts  11.1 us
    all_gather x1, blocking collectives, nearby_x(): lax.all_gather(boundary_rows, 'gx', axis=1, tiled=True)  9.93 us
    reduce_sum x1, other arithmetic, shards(): local_sums = jnp.sum(residual * residual, axis=(1, 2, 3))  7.5 us
    dot_general x3, matrix products, line_solve(): jnp.einsum(patterns[line_axis], inverse, line_field, precision=exact_mode)  7.19 us
    gather x3, local copies, waits for them, and re-layouts, neighbour_table(): return jnp.transpose(padded[:, picked, :], (1, 0, 2))  5.86 us
  transfers between devices with their start and end apart: 6, of which 4 were waited for; matrix products, arithmetic and copies ran while one was open for 13% of the time, Pallas kernels for 0%

commit v1 on v0

v1 whole, which is shorter than its diff:
```python
import functools

import jax
import jax.numpy as jnp
from jax import lax
from jax.experimental import pallas as pl
from jax.experimental.pallas import tpu as pltpu
from jax.sharding import PartitionSpec as P

MESH = pl.DeviceIdType.MESH
HIGHEST = lax.Precision.HIGHEST
gas_ratio = 0.4
courant = 8000.0
damping = 0.0625
fourth_coef = 0.5
AXES = ("gx", "gy", "gz")

NN = (((1,), (0,)), ((), ()))
NT = (((1,), (1,)), ((), ()))
TN = (((0,), (0,)), ((), ()))


def exact_dot(a, b, dims):
    return lax.dot_general(a, b, dims, precision=HIGHEST, preferred_element_type=jnp.float32)


def halves(a):
    high = a.astype(jnp.bfloat16)
    low = (a - high.astype(jnp.float32)).astype(jnp.bfloat16)
    return high, low


def split_dot(a, b, dims):
    def dot(x, y):
        return lax.dot_general(x, y, dims, preferred_element_type=jnp.float32)

    return dot(a[0], b[0]) + (dot(a[0], b[1]) + dot(a[1], b[0]))


def iota(shape, dim):
    return lax.broadcasted_iota(jnp.int32, shape, dim)


def primitives(u):
    inverse = 1.0 / u[0]
    velocity = [u[1] * inverse, u[2] * inverse, u[3] * inverse]
    kinetic = 0.5 * (velocity[0] * velocity[0] + velocity[1] * velocity[1] + velocity[2] * velocity[2])
    internal = jnp.maximum(u[4] * inverse - kinetic, 0.25)
    pressure = gas_ratio * u[0] * internal
    return velocity, internal, pressure


def fluxes(u, direction, values=None):
    velocity, internal, pressure = primitives(u) if values is None else values
    carried = velocity[direction]
    found = [u[1 + direction]]
    for component in range(3):
        moment = u[1 + component] * carried
        if component == direction:
            moment = moment + pressure
        found.append(moment)
    found.append((u[4] + pressure) * carried)
    return found


def coupling(reduced, index, blocks, speed, load):
    inner = jnp.where(index > 0, 1.0, 0.0).astype(jnp.float32)
    outer = jnp.where(index < blocks - 1, 1.0, 0.0).astype(jnp.float32)
    low = jnp.maximum(4 * index - 2, 0)
    high = jnp.minimum(4 * index + 4, 4 * blocks - 2)
    l0 = load(low) * inner
    l1 = load(low + 1) * inner
    f0 = load(high) * outer
    f1 = load(high + 1) * outer
    g0 = fourth_coef * l0 + (-0.5 * speed - 4.0 * fourth_coef) * l1
    g1 = fourth_coef * l1
    h0 = fourth_coef * f0
    h1 = (0.5 * speed - 4.0 * fourth_coef) * f0 + fourth_coef * f1
    return [g0, g1, h0, h1]


def kernel(dims, state, ax, ay, az, rx, sy, sz, ry, rz, adv, out, stats_out,
           uz, uy, hx, res, edge, field, first, xb, yb, zb, stx, sty, stz, khi, klo, azx,
           in_sem, halo_send, halo_recv, xs, xr, ys, yr, zs, zr, ss, sr):
    counts, nv, cz, cy, cx, cells = dims
    gx, gy, gz = counts
    rows = cz * cy
    me = [lax.axis_index(axis) for axis in AXES]

    loads = []
    for v in range(nv):
        copy = pltpu.make_async_copy(state.at[v], uz.at[v, pl.ds(2 * cy, rows)], in_sem.at[v])
        copy.start()
        loads.append(copy)

    barrier = pltpu.get_barrier_semaphore()
    total = 0
    for axis, count, place in zip(AXES, counts, me):
        for k in range(1, count):
            pl.semaphore_signal(barrier, inc=1, device_id={axis: lax.rem(place + k, count)}, device_id_type=MESH)
            total += 1
    for copy in loads:
        copy.wait()
    pl.semaphore_wait(barrier, total)

    def ring(axis, slot, down_src, down_dst, up_src, up_dst):
        count, place = counts[axis], me[axis]
        lower = lax.rem(place + count - 1, count)
        upper = lax.rem(place + 1, count)
        down = pltpu.make_async_remote_copy(
            src_ref=down_src, dst_ref=down_dst, send_sem=halo_send.at[slot], recv_sem=halo_recv.at[slot],
            device_id={AXES[axis]: lower}, device_id_type=MESH)
        up = pltpu.make_async_remote_copy(
            src_ref=up_src, dst_ref=up_dst, send_sem=halo_send.at[slot + 1], recv_sem=halo_recv.at[slot + 1],
            device_id={AXES[axis]: upper}, device_id_type=MESH)
        down.start()
        up.start()
        return [down, up]

    def spread(axis, src, dst, send, recv):
        count, place = counts[axis], me[axis]
        copies = []
        for k in range(1, count):
            copy = pltpu.make_async_remote_copy(
                src_ref=src, dst_ref=dst, send_sem=send(k - 1), recv_sem=recv(k - 1),
                device_id={AXES[axis]: lax.rem(place + k, count)}, device_id_type=MESH)
            copy.start()
            copies.append(copy)
        return copies

    z_halo = ring(2, 4,
                  uz.at[:, pl.ds(2 * cy, 2 * cy)], uz.at[:, pl.ds((cz + 2) * cy, 2 * cy)],
                  uz.at[:, pl.ds(cz * cy, 2 * cy)], uz.at[:, pl.ds(0, 2 * cy)])

    sub8, lane8 = iota((8, cx), 0), iota((8, cx), 1)
    target = jnp.where(sub8 < 2, sub8, cx - 4 + sub8)
    select = jnp.where((sub8 < 4) & (lane8 == target), 1.0, 0.0).astype(jnp.float32)
    for v in range(nv):
        hx[0, v] = exact_dot(select, uz[v, pl.ds(2 * cy, rows), :], NT)
    x_halo = ring(0, 0, hx.at[0], hx.at[1], hx.at[0], hx.at[2])

    for v in range(nv):
        for y in range(cy):
            uy[v, pl.ds((y + 2) * cz, cz), :] = uz[v, pl.ds(2 * cy + y, cz, stride=cy), :]
    y_halo = ring(1, 2,
                  uy.at[:, pl.ds(2 * cz, 2 * cz)], uy.at[:, pl.ds((cy + 2) * cz, 2 * cz)],
                  uy.at[:, pl.ds(cy * cz, 2 * cz)], uy.at[:, pl.ds(0, 2 * cz)])

    spread_z = jnp.where(iota((cz, rows), 1) // cy == iota((cz, rows), 0), 1.0, 0.0).astype(jnp.float32)
    spread_y = jnp.where(lax.rem(iota((cy, rows), 1), cy) == iota((cy, rows), 0), 1.0, 0.0).astype(jnp.float32)
    for v in range(nv):
        azx[...] = exact_dot(az[v], spread_z, NN)
        wide_y = exact_dot(ay[v], spread_y, NN)

        @pl.loop(0, cz)
        def _(z):
            high, low = halves(azx[pl.ds(z, 1), :] * wide_y)
            at = pl.ds(pl.multiple_of(z * cy, cy), cy)
            khi[v, at, :] = high
            klo[v, at, :] = low

    ux = []
    picked = iota((8 * gx, 4 * gx), 0)
    wanted = jnp.where(lax.rem(picked, 8) < 4, (picked // 8) * 4 + lax.rem(picked, 8), -1)
    expand = jnp.where(iota((8 * gx, 4 * gx), 1) == wanted, 1.0, 0.0).astype(jnp.float32)
    sub_m = iota((8, 4 * gx), 0)
    for v in range(nv):
        m = coupling(rx, me[0], gx, adv[0, v], lambda row: rx[v, pl.ds(row, 1), :])
        table = jnp.where(sub_m == 0, m[0], jnp.where(sub_m == 1, m[1], jnp.where(sub_m == 2, m[2],
                          jnp.where(sub_m == 3, m[3], 0.0))))
        columns = exact_dot(select, ax[v], NT)
        ux.append(exact_dot(exact_dot(expand, table, NT), columns, NN))

    def part(u, direction, centre_values=None):
        ahead = fluxes(u[1], direction)
        behind = fluxes(u[-1], direction)
        found = []
        for v in range(nv):
            fourth = u[-2][v] - 4.0 * u[-1][v] + 6.0 * u[0][v] - 4.0 * u[1][v] + u[2][v]
            found.append(-0.5 * (ahead[v] - behind[v]) - damping * fourth)
        return found

    for copy in y_halo:
        copy.wait_recv()

    @pl.loop(0, cy)
    def _(y):
        u = {}
        for off in range(-2, 3):
            at = pl.ds(pl.multiple_of((y + 2 + off) * cz, cz), cz)
            u[off] = [uy[v, at, :] for v in range(nv)]
        found = part(u, 1)
        for v in range(nv):
            res[v, pl.ds(y, cz, stride=cy), :] = found[v]

    for copy in x_halo:
        copy.wait_recv()
    sub_h = iota((8, rows), 0)
    merged = []
    for v in range(nv):
        fill = 1.0 if v == 0 else 0.0
        both = jnp.where(sub_h < 2, hx[1, v], hx[2, v])
        merged.append(jnp.where(sub_h < 4, both, fill))
    halo_flux = fluxes(merged, 0)

    def at_lane(row, lane, value):
        return jnp.where((sub8 == row) & (lane8 == lane), value, 0.0)

    weights = (at_lane(0, cx - 2, -damping) + at_lane(0, cx - 1, 4.0 * damping) + at_lane(1, cx - 1, -damping)
               + at_lane(2, 0, -damping) + at_lane(3, 0, 4.0 * damping) + at_lane(3, 1, -damping)
               + at_lane(4, cx - 1, -0.5) + at_lane(7, 0, 0.5)).astype(jnp.float32)
    for v in range(nv):
        stacked = jnp.where(sub_h < 4, merged[v], pltpu.roll(halo_flux[v], 4, 0))
        edge[v] = exact_dot(stacked, weights, TN)

    for copy in z_halo:
        copy.wait_recv()

    step = 2 * cy
    lane = iota((step, cx), 1)

    def shifted(a, offset):
        moved = pltpu.roll(a, (-offset) % cx, 1)
        inside = lane < cx - offset if offset > 0 else lane >= -offset
        return jnp.where(inside, moved, 0.0)

    def body(i, carry):
        squares, top = carry
        base = pl.multiple_of(i * step, step)
        u = {}
        for off in range(-2, 3):
            at = pl.ds(pl.multiple_of(base + (off + 2) * cy, cy), step)
            u[off] = [uz[v, at, :] for v in range(nv)]
        found = part(u, 2)
        values = primitives(u[0])
        velocity, internal, _ = values
        wave = (jnp.abs(velocity[0]) + jnp.abs(velocity[1]) + jnp.abs(velocity[2])
                + jnp.sqrt(3.0 * 1.4 * gas_ratio * internal))
        top = jnp.maximum(top, wave)
        flux_x = fluxes(u[0], 0, values)
        new_squares = []
        for v in range(nv):
            c = u[0][v]
            fourth = (shifted(c, -2) + shifted(c, 2)) - 4.0 * (shifted(c, -1) + shifted(c, 1)) + 6.0 * c
            along_x = -0.5 * (shifted(flux_x[v], 1) - shifted(flux_x[v], -1)) - damping * fourth
            at = pl.ds(base, step)
            value = res[v, at, :] + found[v] + (along_x + edge[v, at, :])
            res[v, at, :] = value
            new_squares.append(squares[v] + value * value)
        return tuple(new_squares), top

    zero = jnp.zeros((step, cx), jnp.float32)
    squares, top = lax.fori_loop(0, cz // 2, body, ((zero,) * nv, zero))

    x_copies = []
    for v in range(nv):
        parts = halves(res[v])
        across = halves(ax[v])
        xb[v, me[0]] = split_dot(halves(exact_dot(select, ax[v], NN)), parts, NT)
        x_copies.append(spread(0, xb.at[v, me[0]], xb.at[v, me[0]],
                               lambda k: xs.at[v, k], lambda k: xr.at[v, k]))
        first[v] = split_dot(parts, across, NT)

    sub_s = iota((8, cx), 0)
    tile = jnp.where(sub_s == 5, jnp.max(top, axis=0, keepdims=True), 0.0)
    for v in range(nv):
        tile = jnp.where(sub_s == v, jnp.sum(squares[v], axis=0, keepdims=True), tile)
    stx[me[0]] = tile
    stat_copies = [spread(0, stx.at[me[0]], stx.at[me[0]], lambda k: ss.at[0, k], lambda k: sr.at[0, k])]

    def gathered(ref, count):
        result = ref[0]
        for q in range(1, count):
            result = jnp.where(sub_s < nv, result + ref[q], jnp.maximum(result, ref[q]))
        return result

    y_copies = []
    marks_y = (0, 1, cy - 2, cy - 1)
    marks_z = (0, 1, cz - 2, cz - 1)
    for v in range(nv):
        for copy in x_copies[v]:
            copy.wait_recv()
        every = xb[v].reshape(8 * gx, rows)
        solved = first[v] - split_dot(halves(every), halves(ux[v]), TN)
        parts = halves(solved)
        field[v] = split_dot((khi[v], klo[v]), parts, NN)
        for c, mark in enumerate(marks_y):
            yb[v, me[1], pl.ds(c * cz, cz), :] = field[v, pl.ds(mark, cz, stride=cy), :]
        y_copies.append(spread(1, yb.at[v, me[1]], yb.at[v, me[1]],
                               lambda k: ys.at[v, k], lambda k: yr.at[v, k]))

    for copy in stat_copies[0]:
        copy.wait_recv()
    sty[me[1]] = gathered(stx, gx)
    stat_copies.append(spread(1, sty.at[me[1]], sty.at[me[1]], lambda k: ss.at[1, k], lambda k: sr.at[1, k]))

    def combined(reduced, inverse, axis, v, direction, planes, size):
        count = counts[axis]
        sums = [None] * 4
        for j in range(4 * count):
            m = coupling(reduced, me[axis], count, adv[direction, v], lambda row: reduced[v, row, j])
            plane = planes[v, j // 4, pl.ds((j % 4) * size, size), :]
            for c in range(4):
                term = m[c] * plane
                sums[c] = term if sums[c] is None else sums[c] + term
        return sums

    z_copies = []
    for v in range(nv):
        for copy in y_copies[v]:
            copy.wait_recv()
        sums = combined(ry, sy, 1, v, 1, yb, cz)
        for y in range(cy):
            at = pl.ds(y, cz, stride=cy)
            value = field[v, at, :]
            for c, mark in enumerate(marks_y):
                value = value - sy[v, y, mark] * sums[c]
            field[v, at, :] = value
        zb[v, me[2], pl.ds(0, 2 * cy), :] = field[v, pl.ds(0, 2 * cy), :]
        zb[v, me[2], pl.ds(2 * cy, 2 * cy), :] = field[v, pl.ds((cz - 2) * cy, 2 * cy), :]
        z_copies.append(spread(2, zb.at[v, me[2]], zb.at[v, me[2]],
                               lambda k: zs.at[v, k], lambda k: zr.at[v, k]))
        if v == 0:
            for copy in stat_copies[1]:
                copy.wait_recv()
            stz[me[2]] = gathered(sty, gy)
            stat_copies.append(spread(2, stz.at[me[2]], stz.at[me[2]],
                                      lambda k: ss.at[2, k], lambda k: sr.at[2, k]))

    for copy in stat_copies[2]:
        copy.wait_recv()
    final = gathered(stz, gz)
    norm = jnp.sqrt(jnp.sum(final, axis=1, keepdims=True) / float(cells))
    fastest = courant / jnp.max(final, axis=1, keepdims=True)
    stats_out[...] = jnp.where(sub_s < nv, norm, fastest)
    for v in range(nv):
        for copy in z_copies[v]:
            copy.wait_recv()
        sums = combined(rz, sz, 2, v, 2, zb, cy)
        for z in range(cz):
            value = field[v, pl.ds(z * cy, cy), :]
            for c, mark in enumerate(marks_z):
                value = value - sz[v, z, mark] * sums[c]
            out[v, pl.ds(z * cy, cy), :] = value

    for group in [x_halo, y_halo, z_halo] + x_copies + y_copies + z_copies + stat_copies:
        for copy in group:
            copy.wait_send()


def shards(counts, flow_state, advection, inverse_x, inverse_y, inverse_z, reduced_x, reduced_y, reduced_z):
    nv, cz, cy, cx = flow_state.shape
    gx, gy, gz = counts
    rows = cz * cy
    cells = rows * cx * gx * gy * gz
    most = max(counts) - 1
    vmem = pl.BlockSpec(memory_space=pltpu.VMEM)
    smem = pl.BlockSpec(memory_space=pltpu.SMEM)
    f32 = jnp.float32
    dma = pltpu.SemaphoreType.DMA
    out, stats = pl.pallas_call(
        functools.partial(kernel, (counts, nv, cz, cy, cx, cells)),
        out_shape=(jax.ShapeDtypeStruct((nv, rows, cx), f32), jax.ShapeDtypeStruct((8, cx), f32)),
        in_specs=[pl.BlockSpec(memory_space=pl.ANY), vmem, vmem, vmem, vmem, smem, smem, smem, smem, smem],
        out_specs=(vmem, vmem),
        scratch_shapes=[
            pltpu.VMEM((nv, (cz + 4) * cy, cx), f32),
            pltpu.VMEM((nv, (cy + 4) * cz, cx), f32),
            pltpu.VMEM((3, nv, 8, rows), f32),
            pltpu.VMEM((nv, rows, cx), f32),
            pltpu.VMEM((nv, rows, cx), f32),
            pltpu.VMEM((nv, rows, cx), f32),
            pltpu.VMEM((nv, rows, cx), f32),
            pltpu.VMEM((nv, gx, 8, rows), f32),
            pltpu.VMEM((nv, gy, 4 * cz, cx), f32),
            pltpu.VMEM((nv, gz, 4 * cy, cx), f32),
            pltpu.VMEM((gx, 8, cx), f32),
            pltpu.VMEM((gy, 8, cx), f32),
            pltpu.VMEM((gz, 8, cx), f32),
            pltpu.VMEM((nv, rows, rows), jnp.bfloat16),
            pltpu.VMEM((nv, rows, rows), jnp.bfloat16),
            pltpu.VMEM((cz, rows), f32),
            dma((nv,)),
            dma((6,)), dma((6,)),
            dma((nv, gx - 1)), dma((nv, gx - 1)),
            dma((nv, gy - 1)), dma((nv, gy - 1)),
            dma((nv, gz - 1)), dma((nv, gz - 1)),
            dma((3, most)), dma((3, most)),
        ],
        compiler_params=pltpu.CompilerParams(
            collective_id=0, has_side_effects=True, vmem_limit_bytes=60 * 1024 * 1024),
    )(flow_state.reshape(nv, rows, cx), inverse_x, inverse_y, inverse_z, reduced_x, inverse_y, inverse_z,
      reduced_y, reduced_z, advection)
    update = (out * stats[5, 0]).reshape(flow_state.shape)
    return update, stats[:nv, 0]


def solution(mesh):
    counts = tuple(mesh.shape[axis] for axis in AXES)
    placed = (P(None, "gz", "gy", "gx"), P(), P(), P(), P(), P(), P(), P())
    return jax.shard_map(
        functools.partial(shards, counts),
        mesh=mesh,
        in_specs=placed,
        out_specs=(P(None, "gz", "gy", "gx"), P()),
        check_vma=False,
    )
```

time: 201 us -> 55 us (0.27)
  blocking collectives: 112 us -> 0 us
  Pallas kernels: 0 us -> 49.2 us
  local copies, waits for them, and re-layouts: 36.1 us -> 1.82 us
  other arithmetic: 21.9 us -> 3.1 us
  waiting for transfers between devices: 9.47 us -> 0 us
  matrix products: 9.39 us -> 0 us
  starting transfers between devices: 8.59 us -> 0 us
    pallas_call x0 -> x1, Pallas kernels: none -> 49.2 us  [shards(): pl.pallas_call(functools.partial(kernel, (counts, nv, cz, cy, cx, cells))...]
    pmax x1 -> x0, blocking collectives: 40.3 us -> none  [shards(): top_speed = lax.pmax(local_top, ('gx', 'gy', 'gz'))]
    psum x1 -> x0, blocking collectives: 37.8 us -> none  [shards(): squares = lax.psum(local_sums, ('gx', 'gy', 'gz'))]
    all_gather x3 -> x0, blocking collectives: 34.4 us -> none  [the longest x1 21.7 us: nearby_z(): lax.all_gather(boundary_rows, 'gz', axis=1, tiled=True)]
    unnamed x61 -> x2, local copies, waits for them, and re-layouts: 11.1 us -> 0.01 us
    ppermute x6 -> x0, waiting for transfers between devices: 9.47 us -> none  [the longest x3 5.03 us: with_halo(): lax.ppermute(lax.slice_in_dim(block, block.shape[dim] - width, None, axis...]
    dot_general x6 -> x0, matrix products: 9.39 us -> none  [the longest x3 7.19 us: line_solve(): jnp.einsum(patterns[line_axis], inverse, line_field, precision=exact_mode)]
    reduce_sum x5 -> x0, other arithmetic: 8.98 us -> none  [the longest x1 7.5 us: shards(): local_sums = jnp.sum(residual * residual, axis=(1, 2, 3))]
  transfers between devices with their start and end apart: 6 -> 0, of which waited for: 4 -> 0; matrix products, arithmetic and copies ran while one was open for 13% -> 0% of each run, Pallas kernels for 0% -> 0%
where the time goes in v1:
time: 55 us; the launch traced here: 54.7 us
  Pallas kernels  49.2 us (89%)
  other arithmetic  3.1 us (6%)
  local copies, waits for them, and re-layouts  1.82 us (3%)
  between operations  0.64 us (1%)
    pallas_call x1, Pallas kernels, shards(): pl.pallas_call(functools.partial(kernel, (counts, nv, cz, cy, cx, cells))...  49.2 us
    mul x1, other arithmetic, shards(): update = (out * stats[5, 0]).reshape(flow_state.shape)  3.1 us
    slice x1, local copies, waits for them, and re-layouts, shards(): update = (out * stats[5, 0]).reshape(flow_state.shape)  1.19 us

profile of v1, /device:TPU:0, one launch (start us, length us, event | category | flops | bytes accessed | tf_op | source)
XLA Modules:
  0.0 54.7 jit_solution(15399234475119421950)
XLA Ops:
  0.6 49.2 %shard_map.95 = (f32[5,512,128]{2,1,0:T(8,128)}, f32[8,128]{1,0:T(8,128)}) custom-call(f32[5,512,128]{2,1,0:T(8,128)} %bitcast.3, f32[5,128,128]{2,1,0:T(8,128)} %ax.1, f32[5,16,16]{2,1,0:T(8,128)} %sy.1, f32[5,32,32]{2,1,0:T(8,128)} %sz.1, f32[5,16,16]{2,1,0:T(8,128)} %rx.1, f32[5,16,16]{2,1,0:T(8,128)} %sy.1, f32[5,32,32]{2,1,0:T(8,128)} %sz.1, ...), custom_call_target="tpu_custom_call" | custom-call | tf_op jit(solution)/shard_map/pallas_call | solution.py:361
  49.8 1.2 %slice.6 = f32[1,1]{1,0:T(1,128)} slice(f32[8,128]{1,0:T(8,128)} %get-tuple-element.5), slice={[5:6], [0:1]} | slice | bytes 8 | tf_op jit(solution)/shard_map/slice | solution.py:394
  51.0 0.0 copy-start
  51.0 3.1 %broadcast_multiply_fusion = f32[5,512,128]{2,1,0:T(8,128)} fusion(f32[5,512,128]{2,1,0:T(8,128)} %get-tuple-element.4, f32[]{:T(128)} %bitcast.1), kind=kLoop, calls=%fused_computation | loop fusion | flops 327680 | bytes 2621444 | tf_op jit(solution)/shard_map/mul | solution.py:394
  54.1 0.0 copy-done
  54.1 0.6 %slice_reduce_fusion = f32[5]{0:T(128)} fusion(f32[8,128]{1,0:T(8,128)S(1)} %copy-done), kind=kLoop, calls=%fused_computation.1 | loop fusion | bytes 40 | tf_op jit(solution)/shard_map/slice | solution.py:395
Async XLA Ops:
  51.0 3.1 %copy-start = (f32[8,128]{1,0:T(8,128)S(1)}, f32[8,128]{1,0:T(8,128)}, u32[]{:S(2)}) copy-start(f32[8,128]{1,0:T(8,128)} %get-tuple-element.5) | copy-start | bytes 12292

commit v2 on v1

--- a/solution.py
+++ b/solution.py
@@ -79,9 +79,10 @@
     return [g0, g1, h0, h1]
 
 
-def kernel(dims, state, ax, ay, az, rx, sy, sz, ry, rz, adv, out, stats_out,
-           uz, uy, hx, res, edge, field, first, xb, yb, zb, stx, sty, stz, khi, klo, azx,
-           in_sem, halo_send, halo_recv, xs, xr, ys, yr, zs, zr, ss, sr):
+def kernel(dims, state, ax_in, ay_in, az_in, rx_in, ry_in, rz_in, adv, out, rms_out,
+           ax, ay, az, rx, sy, sz, ry, rz,
+           uz, uy, hx, res, edge, field, first, xb, yb, zt, stx, sty, stz, khi, klo, azx,
+           in_sem, table_sem, halo_send, halo_recv, xs, xr, ys, yr, zs, zr, ss, sr):
     counts, nv, cz, cy, cx, cells = dims
     gx, gy, gz = counts
     rows = cz * cy
@@ -92,6 +93,12 @@
         copy = pltpu.make_async_copy(state.at[v], uz.at[v, pl.ds(2 * cy, rows)], in_sem.at[v])
         copy.start()
         loads.append(copy)
+    tables = []
+    for slot, (source, target) in enumerate(((ax_in, ax), (ay_in, ay), (az_in, az), (rx_in, rx),
+                                             (ry_in, ry), (rz_in, rz), (ay_in, sy), (az_in, sz))):
+        copy = pltpu.make_async_copy(source, target, table_sem.at[slot])
+        copy.start()
+        tables.append(copy)
 
     barrier = pltpu.get_barrier_semaphore()
     total = 0
@@ -135,9 +142,19 @@
     sub8, lane8 = iota((8, cx), 0), iota((8, cx), 1)
     target = jnp.where(sub8 < 2, sub8, cx - 4 + sub8)
     select = jnp.where((sub8 < 4) & (lane8 == target), 1.0, 0.0).astype(jnp.float32)
-    for v in range(nv):
-        hx[0, v] = exact_dot(select, uz[v, pl.ds(2 * cy, rows), :], NT)
-    x_halo = ring(0, 0, hx.at[0], hx.at[1], hx.at[0], hx.at[2])
+    sub_h = iota((8, rows), 0)
+    for group in range(0, nv, 4):
+        low = jnp.zeros((8, rows), jnp.float32)
+        high = low
+        for v in range(group, min(group + 4, nv)):
+            place = v - group
+            ends = exact_dot(select, uz[v, pl.ds(2 * cy, rows), :], NT)
+            mine = sub_h // 2 == place
+            low = jnp.where(mine, pltpu.roll(ends, (2 * place) % 8, 0), low)
+            high = jnp.where(mine, pltpu.roll(ends, (2 * place - 2) % 8, 0), high)
+        hx[0, group // 4] = low
+        hx[1, group // 4] = high
+    x_halo = ring(0, 0, hx.at[0], hx.at[2], hx.at[1], hx.at[3])
 
     for v in range(nv):
         for y in range(cy):
@@ -145,6 +162,9 @@
     y_halo = ring(1, 2,
                   uy.at[:, pl.ds(2 * cz, 2 * cz)], uy.at[:, pl.ds((cy + 2) * cz, 2 * cz)],
                   uy.at[:, pl.ds(cy * cz, 2 * cz)], uy.at[:, pl.ds(0, 2 * cz)])
+
+    for copy in tables[:4]:
+        copy.wait()
 
     spread_z = jnp.where(iota((cz, rows), 1) // cy == iota((cz, rows), 0), 1.0, 0.0).astype(jnp.float32)
     spread_y = jnp.where(lax.rem(iota((cy, rows), 1), cy) == iota((cy, rows), 0), 1.0, 0.0).astype(jnp.float32)
@@ -195,11 +215,12 @@
 
     for copy in x_halo:
         copy.wait_recv()
-    sub_h = iota((8, rows), 0)
     merged = []
     for v in range(nv):
         fill = 1.0 if v == 0 else 0.0
-        both = jnp.where(sub_h < 2, hx[1, v], hx[2, v])
+        place = v % 4
+        both = jnp.where(sub_h < 2, pltpu.roll(hx[2, v // 4], (-2 * place) % 8, 0),
+                         pltpu.roll(hx[3, v // 4], (2 - 2 * place) % 8, 0))
         merged.append(jnp.where(sub_h < 4, both, fill))
     halo_flux = fluxes(merged, 0)
 
@@ -305,7 +326,44 @@
                 sums[c] = term if sums[c] is None else sums[c] + term
         return sums
 
+    level, levels = me[2], gz
+    low = jnp.maximum(4 * level - 2, 0)
+    high = jnp.minimum(4 * level + 4, 4 * levels - 2)
+    own = 4 * level
+    has_low, has_high = level > 0, level < levels - 1
     z_copies = []
+    for v in range(nv):
+        up = pltpu.make_async_remote_copy(
+            src_ref=zt.at[v, 0], dst_ref=zt.at[v, 2], send_sem=zs.at[v, 0], recv_sem=zr.at[v, 0],
+            device_id={"gz": jnp.minimum(level + 1, levels - 1)}, device_id_type=MESH)
+        down = pltpu.make_async_remote_copy(
+            src_ref=zt.at[v, 1], dst_ref=zt.at[v, 3], send_sem=zs.at[v, 1], recv_sem=zr.at[v, 1],
+            device_id={"gz": jnp.maximum(level - 1, 0)}, device_id_type=MESH)
+        z_copies.append((up, down))
+
+    def planes_of(v):
+        return [field[v, pl.ds(mark * cy, cy), :] for mark in marks_z]
+
+    def from_own(v, row, planes):
+        return ((rz[v, row, own] * planes[0] + rz[v, row, own + 1] * planes[1])
+                + (rz[v, row, own + 2] * planes[2] + rz[v, row, own + 3] * planes[3]))
+
+    def carrier(v, corner, valid):
+        x00, x01 = rz[v, corner, corner], rz[v, corner, corner + 1]
+        x10, x11 = rz[v, corner + 1, corner], rz[v, corner + 1, corner + 1]
+        inverse = 1.0 / jnp.full((cy, cx), jnp.where(valid, x00 * x11 - x01 * x10, 1.0), jnp.float32)
+
+        def apply(row, pair):
+            a, b = rz[v, row, corner], rz[v, row, corner + 1]
+            return ((a * x11 - b * x10) * pair[0] + (b * x00 - a * x01) * pair[1]) * inverse
+
+        return apply
+
+    def pair_of(v, slot):
+        return [zt[v, slot, pl.ds(0, cy), :], zt[v, slot, pl.ds(cy, cy), :]]
+
+    for copy in tables[4:]:
+        copy.wait()
     for v in range(nv):
         for copy in y_copies[v]:
             copy.wait_recv()
@@ -316,10 +374,21 @@
             for c, mark in enumerate(marks_y):
                 value = value - sy[v, y, mark] * sums[c]
             field[v, at, :] = value
-        zb[v, me[2], pl.ds(0, 2 * cy), :] = field[v, pl.ds(0, 2 * cy), :]
-        zb[v, me[2], pl.ds(2 * cy, 2 * cy), :] = field[v, pl.ds((cz - 2) * cy, 2 * cy), :]
-        z_copies.append(spread(2, zb.at[v, me[2]], zb.at[v, me[2]],
-                               lambda k: zs.at[v, k], lambda k: zr.at[v, k]))
+        planes = planes_of(v)
+        for r in range(2):
+            zt[v, 0, pl.ds(r * cy, cy), :] = from_own(v, own + 2 + r, planes)
+            zt[v, 1, pl.ds(r * cy, cy), :] = from_own(v, own + r, planes)
+
+        @pl.when(level == 0)
+        def _():
+            zt[v, 2] = jnp.zeros((2 * cy, cx), jnp.float32)
+            z_copies[v][0].start()
+
+        @pl.when(level == levels - 1)
+        def _():
+            zt[v, 3] = jnp.zeros((2 * cy, cx), jnp.float32)
+            z_copies[v][1].start()
+
         if v == 0:
             for copy in stat_copies[1]:
                 copy.wait_recv()
@@ -327,25 +396,72 @@
             stat_copies.append(spread(2, stz.at[me[2]], stz.at[me[2]],
                                       lambda k: ss.at[2, k], lambda k: sr.at[2, k]))
 
+    for v in range(nv):
+        up, down = z_copies[v]
+
+        @pl.when(has_low)
+        def _():
+            up.wait_recv()
+
+        @pl.when(has_low & has_high)
+        def _():
+            pair, apply = pair_of(v, 2), carrier(v, low, has_low)
+            for r in range(2):
+                at = pl.ds(r * cy, cy)
+                zt[v, 0, at, :] = zt[v, 0, at, :] + apply(own + 2 + r, pair)
+            up.start()
+
+        @pl.when(has_high)
+        def _():
+            down.wait_recv()
+
+        @pl.when(has_low & has_high)
+        def _():
+            pair, apply = pair_of(v, 3), carrier(v, high, has_high)
+            for r in range(2):
+                at = pl.ds(r * cy, cy)
+                zt[v, 1, at, :] = zt[v, 1, at, :] + apply(own + r, pair)
+            down.start()
+
     for copy in stat_copies[2]:
         copy.wait_recv()
     final = gathered(stz, gz)
     norm = jnp.sqrt(jnp.sum(final, axis=1, keepdims=True) / float(cells))
-    fastest = courant / jnp.max(final, axis=1, keepdims=True)
-    stats_out[...] = jnp.where(sub_s < nv, norm, fastest)
-    for v in range(nv):
-        for copy in z_copies[v]:
-            copy.wait_recv()
-        sums = combined(rz, sz, 2, v, 2, zb, cy)
+    norm = jnp.broadcast_to(norm, (8, cx))
+    for v in range(nv):
+        rms_out[v] = norm[v, 0]
+    fastest = jnp.broadcast_to(courant / jnp.max(final, axis=1, keepdims=True), (8, cx))
+    time_step = jnp.broadcast_to(fastest[5:6, :], (cy, cx))
+    inner = jnp.where(has_low, 1.0, 0.0).astype(jnp.float32)
+    outer = jnp.where(has_high, 1.0, 0.0).astype(jnp.float32)
+    for v in range(nv):
+        planes = planes_of(v)
+        below, above = pair_of(v, 2), pair_of(v, 3)
+        lift, sink = carrier(v, low, has_low), carrier(v, high, has_high)
+        l = [inner * (below[r] + from_own(v, low + r, planes) + sink(low + r, above)) for r in range(2)]
+        f = [outer * (above[r] + from_own(v, high + r, planes) + lift(high + r, below)) for r in range(2)]
+        speed = adv[2, v]
+        sums = [fourth_coef * l[0] + (-0.5 * speed - 4.0 * fourth_coef) * l[1],
+                fourth_coef * l[1],
+                fourth_coef * f[0],
+                (0.5 * speed - 4.0 * fourth_coef) * f[0] + fourth_coef * f[1]]
         for z in range(cz):
             value = field[v, pl.ds(z * cy, cy), :]
             for c, mark in enumerate(marks_z):
                 value = value - sz[v, z, mark] * sums[c]
-            out[v, pl.ds(z * cy, cy), :] = value
-
-    for group in [x_halo, y_halo, z_halo] + x_copies + y_copies + z_copies + stat_copies:
+            out[v, pl.ds(z * cy, cy), :] = value * time_step
+
+    for group in [x_halo, y_halo, z_halo] + x_copies + y_copies + stat_copies:
         for copy in group:
             copy.wait_send()
+    for v in range(nv):
+        @pl.when(has_high)
+        def _():
+            z_copies[v][0].wait_send()
+
+        @pl.when(has_low)
+        def _():
+            z_copies[v][1].wait_send()
 
 
 def shards(counts, flow_state, advection, inverse_x, inverse_y, inverse_z, reduced_x, reduced_y, reduced_z):
@@ -358,41 +474,49 @@
     smem = pl.BlockSpec(memory_space=pltpu.SMEM)
     f32 = jnp.float32
     dma = pltpu.SemaphoreType.DMA
-    out, stats = pl.pallas_call(
+    hbm = pl.BlockSpec(memory_space=pl.ANY)
+    out, rms = pl.pallas_call(
         functools.partial(kernel, (counts, nv, cz, cy, cx, cells)),
-        out_shape=(jax.ShapeDtypeStruct((nv, rows, cx), f32), jax.ShapeDtypeStruct((8, cx), f32)),
-        in_specs=[pl.BlockSpec(memory_space=pl.ANY), vmem, vmem, vmem, vmem, smem, smem, smem, smem, smem],
-        out_specs=(vmem, vmem),
+        out_shape=(jax.ShapeDtypeStruct((nv, rows, cx), f32), jax.ShapeDtypeStruct((nv,), f32)),
+        in_specs=[hbm] * 7 + [smem],
+        out_specs=(vmem, smem),
         scratch_shapes=[
+            pltpu.VMEM(inverse_x.shape, f32),
+            pltpu.VMEM(inverse_y.shape, f32),
+            pltpu.VMEM(inverse_z.shape, f32),
+            pltpu.VMEM(reduced_x.shape, f32),
+            pltpu.SMEM(inverse_y.shape, f32),
+            pltpu.SMEM(inverse_z.shape, f32),
+            pltpu.SMEM(reduced_y.shape, f32),
+            pltpu.SMEM(reduced_z.shape, f32),
             pltpu.VMEM((nv, (cz + 4) * cy, cx), f32),
             pltpu.VMEM((nv, (cy + 4) * cz, cx), f32),
-            pltpu.VMEM((3, nv, 8, rows), f32),
+            pltpu.VMEM((4, -(-nv // 4), 8, rows), f32),
             pltpu.VMEM((nv, rows, cx), f32),
             pltpu.VMEM((nv, rows, cx), f32),
             pltpu.VMEM((nv, rows, cx), f32),
             pltpu.VMEM((nv, rows, cx), f32),
             pltpu.VMEM((nv, gx, 8, rows), f32),
             pltpu.VMEM((nv, gy, 4 * cz, cx), f32),
-            pltpu.VMEM((nv, gz, 4 * cy, cx), f32),
+            pltpu.VMEM((nv, 4, 2 * cy, cx), f32),
             pltpu.VMEM((gx, 8, cx), f32),
             pltpu.VMEM((gy, 8, cx), f32),
             pltpu.VMEM((gz, 8, cx), f32),
             pltpu.VMEM((nv, rows, rows), jnp.bfloat16),
             pltpu.VMEM((nv, rows, rows), jnp.bfloat16),
             pltpu.VMEM((cz, rows), f32),
-            dma((nv,)),
+            dma((nv,)), dma((8,)),
             dma((6,)), dma((6,)),
             dma((nv, gx - 1)), dma((nv, gx - 1)),
             dma((nv, gy - 1)), dma((nv, gy - 1)),
-            dma((nv, gz - 1)), dma((nv, gz - 1)),
+            dma((nv, 2)), dma((nv, 2)),
             dma((3, most)), dma((3, most)),
         ],
         compiler_params=pltpu.CompilerParams(
             collective_id=0, has_side_effects=True, vmem_limit_bytes=60 * 1024 * 1024),
-    )(flow_state.reshape(nv, rows, cx), inverse_x, inverse_y, inverse_z, reduced_x, inverse_y, inverse_z,
-      reduced_y, reduced_z, advection)
-    update = (out * stats[5, 0]).reshape(flow_state.shape)
-    return update, stats[:nv, 0]
+    )(flow_state.reshape(nv, rows, cx), inverse_x, inverse_y, inverse_z, reduced_x, reduced_y, reduced_z,
+      advection)
+    return out.reshape(flow_state.shape), rms
 
 
 def solution(mesh):

time: 55 us -> 68.8 us (1.25)
  Pallas kernels: 49.2 us -> 64.9 us
  other arithmetic: 3.1 us -> 0 us
  local copies, waits for them, and re-layouts: 1.82 us -> 3.02 us
    pallas_call x1, Pallas kernels: 49.2 us -> 64.9 us  [shards(): pl.pallas_call(functools.partial(kernel, (counts, nv, cz, cy, cx, cells))...]
    mul x1 -> x0, other arithmetic: 3.1 us -> none  [shards(): update = (out * stats[5, 0]).reshape(flow_state.shape)]
    unnamed x2 -> x4, local copies, waits for them, and re-layouts: 0.01 us -> 3.02 us
    slice x2 -> x0, local copies, waits for them, and re-layouts: 1.82 us -> none  [the longest x1 1.19 us: shards(): update = (out * stats[5, 0]).reshape(flow_state.shape)]
where the time goes in v2:
time: 68.8 us; the launch traced here: 68.6 us
  Pallas kernels  64.9 us (94%)
  local copies, waits for them, and re-layouts  3.02 us (4%)
    pallas_call x1, Pallas kernels, shards(): pl.pallas_call(functools.partial(kernel, (counts, nv, cz, cy, cx, cells))...  64.9 us
    unnamed x4, local copies, waits for them, and re-layouts  3.02 us

profile of v2, /device:TPU:0, one launch (start us, length us, event | category | flops | bytes accessed | tf_op | source)
XLA Modules:
  0.0 68.6 jit_solution(1997545934138987250)
XLA Ops:
  0.6 64.9 %shard_map.95 = (f32[5,512,128]{2,1,0:T(8,128)}, f32[5]{0:T(128)}) custom-call(f32[5,512,128]{2,1,0:T(8,128)} %bitcast.2, f32[5,128,128]{2,1,0:T(8,128)} %ax_in.1, f32[5,16,16]{2,1,0:T(8,128)} %ay_in.1, f32[5,32,32]{2,1,0:T(8,128)} %az_in.1, f32[5,16,16]{2,1,0:T(8,128)} %rx_in.1, f32[5,8,8]{2,1,0:T(8,128)} %ry_in.1, f32[5,16,16]{2,1,0:T(8,128)} %rz_in.1, ...), custom_call_target="tpu_custom_call" | custom-call | tf_op jit(solution)/shard_map/pallas_call | solution.py:478
  65.6 0.0 copy-start
  65.6 2.5 %copy.12 = f32[5,32,16,128]{3,2,1,0:T(8,128)} copy(f32[5,32,16,128]{3,2,1,0:T(8,128)} %bitcast.3) | data formatting | bytes 2621440
  68.1 0.0 copy-done
  68.1 0.5 copy.13
Async XLA Ops:
  65.6 2.5 %copy-start = (f32[5]{0:T(128)S(1)}, f32[5]{0:T(128)}, u32[]{:S(2)}) copy-start(f32[5]{0:T(128)} %get-tuple-element.9) | copy-start | bytes 64

commit v3 on v2

--- a/solution.py
+++ b/solution.py
@@ -396,32 +396,34 @@
             stat_copies.append(spread(2, stz.at[me[2]], stz.at[me[2]],
                                       lambda k: ss.at[2, k], lambda k: sr.at[2, k]))
 
-    for v in range(nv):
-        up, down = z_copies[v]
-
-        @pl.when(has_low)
+    def relay(v, way):
+        copy = z_copies[v][way]
+        corner, valid, row = ((low, has_low, own + 2), (high, has_high, own))[way]
+
+        @pl.when(valid)
         def _():
-            up.wait_recv()
+            copy.wait_recv()
 
         @pl.when(has_low & has_high)
         def _():
-            pair, apply = pair_of(v, 2), carrier(v, low, has_low)
+            pair, apply = pair_of(v, 2 + way), carrier(v, corner, valid)
             for r in range(2):
                 at = pl.ds(r * cy, cy)
-                zt[v, 0, at, :] = zt[v, 0, at, :] + apply(own + 2 + r, pair)
-            up.start()
-
-        @pl.when(has_high)
-        def _():
-            down.wait_recv()
-
-        @pl.when(has_low & has_high)
-        def _():
-            pair, apply = pair_of(v, 3), carrier(v, high, has_high)
-            for r in range(2):
-                at = pl.ds(r * cy, cy)
-                zt[v, 1, at, :] = zt[v, 1, at, :] + apply(own + r, pair)
-            down.start()
+                zt[v, way, at, :] = zt[v, way, at, :] + apply(row + r, pair)
+            copy.start()
+
+    def relay_all(ways):
+        for way in ways:
+            for v in range(nv):
+                relay(v, way)
+
+    @pl.when(2 * level < levels)
+    def _():
+        relay_all((0, 1))
+
+    @pl.when(2 * level >= levels)
+    def _():
+        relay_all((1, 0))
 
     for copy in stat_copies[2]:
         copy.wait_recv()

time: 68.8 us -> 44.8 us (0.65)
  Pallas kernels: 64.9 us -> 40.9 us
    pallas_call x1, Pallas kernels: 64.9 us -> 40.9 us  [shards(): pl.pallas_call(functools.partial(kernel, (counts, nv, cz, cy, cx, cells))...]
where the time goes in v3:
time: 44.8 us; the launch traced here: 44.6 us
  Pallas kernels  40.9 us (91%)
  local copies, waits for them, and re-layouts  3.02 us (7%)
  between operations  0.65 us (1%)
    pallas_call x1, Pallas kernels, shards(): pl.pallas_call(functools.partial(kernel, (counts, nv, cz, cy, cx, cells))...  40.9 us
    unnamed x4, local copies, waits for them, and re-layouts  3.02 us

profile of v3, /device:TPU:0, one launch (start us, length us, event | category | flops | bytes accessed | tf_op | source)
XLA Modules:
  0.0 44.6 jit_solution(5534288798328727268)
XLA Ops:
  0.6 40.9 %shard_map.95 = (f32[5,512,128]{2,1,0:T(8,128)}, f32[5]{0:T(128)}) custom-call(f32[5,512,128]{2,1,0:T(8,128)} %bitcast.2, f32[5,128,128]{2,1,0:T(8,128)} %ax_in.1, f32[5,16,16]{2,1,0:T(8,128)} %ay_in.1, f32[5,32,32]{2,1,0:T(8,128)} %az_in.1, f32[5,16,16]{2,1,0:T(8,128)} %rx_in.1, f32[5,8,8]{2,1,0:T(8,128)} %ry_in.1, f32[5,16,16]{2,1,0:T(8,128)} %rz_in.1, ...), custom_call_target="tpu_custom_call" | custom-call | tf_op jit(solution)/shard_map/pallas_call | solution.py:480
  41.6 0.0 copy-start
  41.6 2.5 %copy.12 = f32[5,32,16,128]{3,2,1,0:T(8,128)} copy(f32[5,32,16,128]{3,2,1,0:T(8,128)} %bitcast.3) | data formatting | bytes 2621440
  44.1 0.0 copy-done
  44.1 0.5 %copy.13 = f32[5]{0:T(128)} copy(f32[5]{0:T(128)S(1)} %copy-done) | data formatting | bytes 40
Async XLA Ops:
  41.6 2.5 %copy-start = (f32[5]{0:T(128)S(1)}, f32[5]{0:T(128)}, u32[]{:S(2)}) copy-start(f32[5]{0:T(128)} %get-tuple-element.9) | copy-start | bytes 64
